TPU v7x, 32 devices: a whole 2x2x4 slice. The times are simulated.
32 devices in a mesh: outer: 2 (over y), inner: 4 (over x, core), heads: 4 (over z).
Axes of the slice: x: 2, y: 2, z: 4, core: 2. Of those that a mesh axis runs over, the one named last changes fastest.
Arguments:
- raw_keys: bfloat16 [8, 4096, 8, 128], P(None, ('outer', 'inner'), 'heads'), may hold values from -6 to 6
- raw_values: bfloat16 [8, 4096, 8, 128], P(None, ('outer', 'inner'), 'heads'), may hold values from -6 to 6
- turn_angle: float32 [4096, 64], replicated, may hold values from -3.140625 to 3.140625
Outputs:
- stored_keys: bfloat16 [8, 4096, 8, 128], P(('outer', 'inner'), None, 'heads')
- stored_values: bfloat16 [8, 4096, 8, 128], P(('outer', 'inner'), None, 'heads')
- page_high: bfloat16 [8, 64, 8, 128], P(('outer', 'inner'), None, 'heads')
- page_low: bfloat16 [8, 64, 8, 128], P(('outer', 'inner'), None, 'heads')
All inputs are finite; a program needn't handle non-finite values.
Results may differ from a plain program's by a relative error of at most 0.001.
Values may be sent and summed in bfloat16 or wider, within the bound.
A program may use at most 128 MiB of HBM per device.

v0:
```python
import functools

import jax
import jax.numpy as jnp
from jax import lax
from jax.experimental import pallas as pl
from jax.experimental.pallas import tpu as pltpu
from jax.sharding import PartitionSpec as P

PAGE = 64
MESH = pl.DeviceIdType.MESH


def offsets(outer, inner):
    cores = 2 if inner % 2 == 0 else 1
    chips = inner // cores
    steps = [
        (do, dx, dc)
        for dc in range(cores)
        for do in range(outer)
        for dx in range(chips)
        if (do, dx, dc) != (0, 0, 0)
    ]
    return cores, chips, sorted(steps, key=lambda s: (s[0] != 0) + (s[1] != 0))


def kernel(
    outer, inner, heads,
    keys, values, angle,
    out_keys, out_values, out_high, out_low,
    landed, angles, table, wide, turned, bound,
    send_k, recv_k, send_v, recv_v, local,
):
    group = outer * inner
    batch, rows, size = keys.shape
    own = batch // group
    length = rows // heads
    half = size // 2
    pages = length // PAGE
    cores, chips, steps = offsets(outer, inner)
    o, i = lax.axis_index("outer"), lax.axis_index("inner")
    x, c = i // cores, i % cores
    me = o * inner + i

    def partner(step, sign):
        do, dx, dc = step
        po = (o + sign * do + outer) % outer
        pi = (x + sign * dx + chips) % chips * cores + (c + sign * dc + cores) % cores
        return po, pi

    get_angles = pltpu.make_async_copy(angle, angles, local.at[0])
    get_angles.start()
    mine = pl.ds(pl.multiple_of(me * rows, rows), rows)
    own_keys = pltpu.make_async_copy(
        keys.at[pl.ds(me * own, own)], landed.at[:, mine], local.at[1]
    )
    own_values = pltpu.make_async_copy(
        values.at[pl.ds(me * own, own)], out_values.at[:, mine], local.at[2]
    )
    own_keys.start()
    own_values.start()

    barrier = pltpu.get_barrier_semaphore()
    for step in steps:
        po, pi = partner(step, 1)
        pl.semaphore_signal(
            barrier, inc=1, device_id={"outer": po, "inner": pi}, device_id_type=MESH
        )
    pl.semaphore_wait(barrier, len(steps))

    copies_k, copies_v = [], []
    for j, step in enumerate(steps):
        po, pi = partner(step, 1)
        theirs = pl.ds((po * inner + pi) * own, own)
        for copies, src, dst, send, recv in (
            (copies_k, keys, landed, send_k, recv_k),
            (copies_v, values, out_values, send_v, recv_v),
        ):
            copies.append(
                pltpu.make_async_remote_copy(
                    src_ref=src.at[theirs],
                    dst_ref=dst.at[:, mine],
                    send_sem=send.at[j],
                    recv_sem=recv.at[j],
                    device_id={"outer": po, "inner": pi},
                    device_id_type=MESH,
                )
            )
    far = [(s[0] != 0) + (s[1] != 0) for s in steps]
    for distance in sorted(set(far)):
        for copies in (copies_k, copies_v):
            for j, copy in enumerate(copies):
                if far[j] == distance:
                    copy.start()

    get_angles.wait()

    def fill(p, carry):
        at = pl.ds(pl.multiple_of(p * size, size), size)
        a = angles[:, at]
        table[at] = jnp.concatenate([jnp.cos(a), jnp.sin(a)], axis=0).T
        return carry

    lax.fori_loop(0, table.shape[0] // size, fill, 0)

    def turn(source):
        for n in range(own):
            def page(p, carry):
                at = pl.multiple_of(source * length + p * PAGE, PAGE)
                tab = table[pl.ds(at, PAGE)]
                swap = pltpu.roll(tab, half, 1)
                low_half = lax.broadcasted_iota(jnp.int32, tab.shape, 1) < half
                cosine = jnp.where(low_half, tab, swap)
                sine = jnp.where(low_half, -swap, tab)
                at_rows = pl.ds(pl.multiple_of(at * heads, PAGE * heads), PAGE * heads)
                wide[...] = landed[n, at_rows].astype(jnp.float32)
                for h in range(heads):
                    v = wide[pl.ds(h, PAGE, stride=heads)]
                    y = v * cosine + pltpu.roll(v, half, 1) * sine
                    turned[pl.ds(h, PAGE, stride=heads)] = y
                    bound[0, pl.ds(p * heads + h, 1)] = jnp.max(y, axis=0, keepdims=True)
                    bound[1, pl.ds(p * heads + h, 1)] = jnp.min(y, axis=0, keepdims=True)
                out_keys[n, at_rows] = turned[...].astype(out_keys.dtype)
                return carry

            lax.fori_loop(0, pages, page, 0)
            at_pages = pl.ds(pl.multiple_of(source * pages * heads, pages * heads), pages * heads)
            out_high[n, at_pages] = bound[0].astype(out_high.dtype)
            out_low[n, at_pages] = bound[1].astype(out_low.dtype)

    own_keys.wait()
    turn(me)
    for j, step in enumerate(steps):
        copies_k[j].wait_recv()
        po, pi = partner(step, -1)
        turn(po * inner + pi)
    own_values.wait()
    for j in range(len(steps)):
        copies_v[j].wait_recv()
    for j in range(len(steps)):
        copies_k[j].wait_send()
        copies_v[j].wait_send()


def in_hbm(array):
    return pltpu.with_memory_space_constraint(array, pltpu.HBM)


def store(*refs):
    count = len(refs) // 2
    sems = refs[-1]
    copies = [
        pltpu.make_async_copy(refs[k], refs[count + k], sems.at[k]) for k in range(count)
    ]
    for copy in copies:
        copy.start()
    for copy in copies:
        copy.wait()


def per_device(outer, inner, raw_keys, raw_values, turn_angle):
    batch, length, heads, size = raw_keys.shape
    group = outer * inner
    own, rows, pages = batch // group, length * heads, length // PAGE
    bf16, f32 = jnp.bfloat16, jnp.float32
    scratch_bytes = group * length * size * (2 * own * heads + 8) + 2**22
    outs = pl.pallas_call(
        functools.partial(kernel, outer, inner, heads),
        out_shape=(
            pltpu.VMEM((own, group * rows, size), bf16),
            pltpu.VMEM((own, group * rows, size), bf16),
            pltpu.VMEM((own, group * pages * heads, size), bf16),
            pltpu.VMEM((own, group * pages * heads, size), bf16),
        ),
        in_specs=[pl.BlockSpec(memory_space=pltpu.HBM)] * 3,
        out_specs=[pl.BlockSpec(memory_space=pltpu.VMEM)] * 4,
        scratch_shapes=[
            pltpu.VMEM((own, group * rows, size), bf16),
            pltpu.VMEM((turn_angle.shape[1], turn_angle.shape[0]), f32),
            pltpu.VMEM((turn_angle.shape[0], size), f32),
            pltpu.VMEM((PAGE * heads, size), f32),
            pltpu.VMEM((PAGE * heads, size), f32),
            pltpu.VMEM((2, pages * heads, size), f32),
            pltpu.SemaphoreType.DMA((group,)),
            pltpu.SemaphoreType.DMA((group,)),
            pltpu.SemaphoreType.DMA((group,)),
            pltpu.SemaphoreType.DMA((group,)),
            pltpu.SemaphoreType.DMA((3,)),
        ],
        compiler_params=pltpu.CompilerParams(
            collective_id=0, has_side_effects=True, vmem_limit_bytes=scratch_bytes
        ),
    )(
        in_hbm(raw_keys.reshape(batch, rows, size)),
        in_hbm(raw_values.reshape(batch, rows, size)),
        in_hbm(turn_angle.T),
    )
    keys, values, high, low = pl.pallas_call(
        store,
        out_shape=[jax.ShapeDtypeStruct(out.shape, out.dtype) for out in outs],
        in_specs=[pl.BlockSpec(memory_space=pltpu.VMEM)] * 4,
        out_specs=[pl.BlockSpec(memory_space=pltpu.HBM)] * 4,
        scratch_shapes=[pltpu.SemaphoreType.DMA((4,))],
        compiler_params=pltpu.CompilerParams(vmem_limit_bytes=2**20),
    )(*outs)
    return (
        keys.reshape(own, group * length, heads, size),
        values.reshape(own, group * length, heads, size),
        high.reshape(own, group * pages, heads, size),
        low.reshape(own, group * pages, heads, size),
    )


def solution(mesh):
    moved = P(None, ("outer", "inner"), "heads", None)
    whole = P(("outer", "inner"), None, "heads", None)
    return jax.shard_map(
        functools.partial(per_device, mesh.shape["outer"], mesh.shape["inner"]),
        mesh=mesh,
        in_specs=(moved, moved, P()),
        out_specs=(whole,) * 4,
        check_vma=False,
    )
```

profile of v0, /device:TPU:1, one launch (start us, length us, event | category | flops | bytes accessed | tf_op | source)
XLA Modules:
  0.0 53.0 jit_solution(4901813396964455963)
XLA Ops:
  0.6 50.4 %shard_map.66 = (bf16[1,8192,128]{2,1,0:T(8,128)(2,1)S(1)}, bf16[1,8192,128]{2,1,0:T(8,128)(2,1)S(1)}, bf16[1,128,128]{2,1,0:T(8,128)(2,1)S(1)}, bf16[1,128,128]{2,1,0:T(8,128)(2,1)S(1)}) custom-call(bf16[8,1024,128]{2,1,0:T(8,128)(2,1)} %bitcast.7, bf16[8,1024,128]{2,1,0:T(8,128)(2,1)} %bitcast.8, f32[64,4096]{1,0:T(8,128)} %bitcast.9), custom_call_target="tpu_custom_call" | custom-call | tf_op jit(solution)/shard_map/pallas_call | solution.py:167
  51.0 2.1 %shard_map.67 = (bf16[1,8192,128]{2,1,0:T(8,128)(2,1)}, bf16[1,8192,128]{2,1,0:T(8,128)(2,1)}, bf16[1,128,128]{2,1,0:T(8,128)(2,1)}, bf16[1,128,128]{2,1,0:T(8,128)(2,1)}) custom-call(bf16[1,8192,128]{2,1,0:T(8,128)(2,1)S(1)} %get-tuple-element.12.refs_0_, bf16[1,8192,128]{2,1,0:T(8,128)(2,1)S(1)} %get-tuple-element.13.refs_1_, ...), custom_call_target="tpu_custom_call" | custom-call | tf_op jit(solution)/shard_map/pallas_call | solution.py:198
where the time goes:
time: 53.3 us; the launch traced here: 53 us
  Pallas kernels  52.4 us (98%)
  between operations  0.64 us (1%)
    pallas_call x1, Pallas kernels, per_device(): pl.pallas_call(functools.partial(kernel, outer, inner, heads), out_shape=...  50.4 us
    pallas_call x1, Pallas kernels, per_device(): pl.pallas_call(store, out_shape=[jax.ShapeDtypeStruct(out.shape, out.dtyp...  2.05 us

commit v1 on v0

--- a/solution.py
+++ b/solution.py
@@ -9,6 +9,11 @@
 
 PAGE = 64
 MESH = pl.DeviceIdType.MESH
+
+FIRST = (("YX", "kv"),)
+EVEN = (("Dd", "kv"), ("Yy", "kv"), ("c", "k"), ("Xx", "kv"), ("c", "v"))
+ODD = (("xy", "kv"), ("c", "k"), ("Dd", "kv"), ("c", "v"))
+TURNS = "YXDdxyc"
 
 
 def offsets(outer, inner):
@@ -21,7 +26,23 @@
         for dx in range(chips)
         if (do, dx, dc) != (0, 0, 0)
     ]
-    return cores, chips, sorted(steps, key=lambda s: (s[0] != 0) + (s[1] != 0))
+    return cores, chips, steps
+
+
+def kind(step):
+    name = ("c", "x", "y", "d")[(step[1] != 0) + 2 * (step[0] != 0)]
+    return name if step[2] or name == "c" else name.upper()
+
+
+def queue(steps, spec):
+    return [
+        (j, tensor)
+        for kinds, tensors in spec
+        for tensor in tensors
+        for name in kinds
+        for j, step in enumerate(steps)
+        if kind(step) == name
+    ]
 
 
 def kernel(
@@ -29,7 +50,7 @@
     keys, values, angle,
     out_keys, out_values, out_high, out_low,
     landed, angles, table, wide, turned, bound,
-    send_k, recv_k, send_v, recv_v, local,
+    send_k, recv_k, send_v, recv_v, ready, local,
 ):
     group = outer * inner
     batch, rows, size = keys.shape
@@ -48,8 +69,23 @@
         pi = (x + sign * dx + chips) % chips * cores + (c + sign * dc + cores) % cores
         return po, pi
 
+    def tell(sem, kinds):
+        for step in steps:
+            if kind(step) in kinds:
+                po, pi = partner(step, -1)
+                pl.semaphore_signal(
+                    sem, inc=1, device_id={"outer": po, "inner": pi}, device_id_type=MESH
+                )
+
+    square = (outer, chips, cores) == (2, 2, 2)
+    barrier = pltpu.get_barrier_semaphore()
+    if square:
+        pl.when((c == 1) & (o + x < 2))(lambda: tell(barrier, "XY"))
+        pl.when(c == 1)(lambda: tell(barrier, "c"))
+    else:
+        tell(barrier, "cxydXYD")
+
     get_angles = pltpu.make_async_copy(angle, angles, local.at[0])
-    get_angles.start()
     mine = pl.ds(pl.multiple_of(me * rows, rows), rows)
     own_keys = pltpu.make_async_copy(
         keys.at[pl.ds(me * own, own)], landed.at[:, mine], local.at[1]
@@ -57,41 +93,68 @@
     own_values = pltpu.make_async_copy(
         values.at[pl.ds(me * own, own)], out_values.at[:, mine], local.at[2]
     )
-    own_keys.start()
-    own_values.start()
-
-    barrier = pltpu.get_barrier_semaphore()
-    for step in steps:
-        po, pi = partner(step, 1)
-        pl.semaphore_signal(
-            barrier, inc=1, device_id={"outer": po, "inner": pi}, device_id_type=MESH
-        )
-    pl.semaphore_wait(barrier, len(steps))
-
-    copies_k, copies_v = [], []
+
+    copies = {}
     for j, step in enumerate(steps):
         po, pi = partner(step, 1)
         theirs = pl.ds((po * inner + pi) * own, own)
-        for copies, src, dst, send, recv in (
-            (copies_k, keys, landed, send_k, recv_k),
-            (copies_v, values, out_values, send_v, recv_v),
+        for tensor, src, dst, send, recv in (
+            ("k", keys, landed, send_k, recv_k),
+            ("v", values, out_values, send_v, recv_v),
         ):
-            copies.append(
-                pltpu.make_async_remote_copy(
-                    src_ref=src.at[theirs],
-                    dst_ref=dst.at[:, mine],
-                    send_sem=send.at[j],
-                    recv_sem=recv.at[j],
-                    device_id={"outer": po, "inner": pi},
-                    device_id_type=MESH,
-                )
+            copies[j, tensor] = pltpu.make_async_remote_copy(
+                src_ref=src.at[theirs],
+                dst_ref=dst.at[:, mine],
+                send_sem=send.at[j],
+                recv_sem=recv.at[j],
+                device_id={"outer": po, "inner": pi},
+                device_id_type=MESH,
             )
-    far = [(s[0] != 0) + (s[1] != 0) for s in steps]
-    for distance in sorted(set(far)):
-        for copies in (copies_k, copies_v):
-            for j, copy in enumerate(copies):
-                if far[j] == distance:
-                    copy.start()
+
+    def issue(spec, names="cxydXYD"):
+        for j, tensor in queue(steps, spec):
+            if kind(steps[j]) in names:
+                copies[j, tensor].start()
+
+    if square:
+        pl.semaphore_wait(barrier, 1 + c * ((o + x + 1) % 2))
+
+        @pl.when((c == 1) & (o + x == 2))
+        def _():
+            tell(ready.at[0], "XY")
+
+        @pl.when((c == 1) & (o + x != 1))
+        def _():
+            issue(FIRST)
+
+        for near, far, at in (("X", "Y", 1), ("Y", "X", 0)):
+            @pl.when((c == 1) & (o + x == 1) & (x == at))
+            def _(near=near, far=far):
+                issue(FIRST, near)
+                pl.semaphore_wait(ready.at[0], 1)
+                issue(FIRST, far)
+
+        @pl.when(c == 1)
+        def _():
+            pl.semaphore_wait(ready.at[1], 1)
+            for stage in (2, 3):
+                tell(ready.at[stage], "XY")
+                pl.semaphore_wait(ready.at[stage], 2)
+            tell(ready.at[1], "c")
+
+        @pl.when(c == 0)
+        def _():
+            tell(ready.at[1], "c")
+            pl.semaphore_wait(ready.at[1], 1)
+    else:
+        pl.semaphore_wait(barrier, len(steps))
+        pl.when(c == 1)(lambda: issue(FIRST))
+
+    get_angles.start()
+    own_keys.start()
+    own_values.start()
+    pl.when(c == 0)(lambda: issue(EVEN))
+    pl.when(c == 1)(lambda: issue(ODD))
 
     get_angles.wait()
 
@@ -130,16 +193,15 @@
 
     own_keys.wait()
     turn(me)
-    for j, step in enumerate(steps):
-        copies_k[j].wait_recv()
-        po, pi = partner(step, -1)
+    for j, _ in queue(steps, ((TURNS, "k"),)):
+        copies[j, "k"].wait_recv()
+        po, pi = partner(steps[j], -1)
         turn(po * inner + pi)
     own_values.wait()
     for j in range(len(steps)):
-        copies_v[j].wait_recv()
-    for j in range(len(steps)):
-        copies_k[j].wait_send()
-        copies_v[j].wait_send()
+        copies[j, "v"].wait_recv()
+    for copy in copies.values():
+        copy.wait_send()
 
 
 def in_hbm(array):
@@ -185,6 +247,7 @@
             pltpu.SemaphoreType.DMA((group,)),
             pltpu.SemaphoreType.DMA((group,)),
             pltpu.SemaphoreType.DMA((group,)),
+            pltpu.SemaphoreType.REGULAR((4,)),
             pltpu.SemaphoreType.DMA((3,)),
         ],
         compiler_params=pltpu.CompilerParams(

time: 53.3 us -> 51.6 us (0.968)
  Pallas kernels: 52.4 us -> 50.8 us
    pallas_call x1, Pallas kernels: 50.4 us -> 48.7 us  [per_device(): pl.pallas_call(functools.partial(kernel, outer, inner, heads), out_shape=...]
where the time goes in v1:
time: 51.6 us; the launch traced here: 51.4 us
  Pallas kernels  50.8 us (98%)
  between operations  0.64 us (1%)
    pallas_call x1, Pallas kernels, per_device(): pl.pallas_call(functools.partial(kernel, outer, inner, heads), out_shape=...  48.7 us
    pallas_call x1, Pallas kernels, per_device(): pl.pallas_call(store, out_shape=[jax.ShapeDtypeStruct(out.shape, out.dtyp...  2.05 us

profile of v1, /device:TPU:1, one launch (start us, length us, event | category | flops | bytes accessed | tf_op | source)
XLA Modules:
  0.0 51.4 jit_solution(7475381978509143803)
XLA Ops:
  0.6 48.7 %shard_map.66 = (bf16[1,8192,128]{2,1,0:T(8,128)(2,1)S(1)}, bf16[1,8192,128]{2,1,0:T(8,128)(2,1)S(1)}, bf16[1,128,128]{2,1,0:T(8,128)(2,1)S(1)}, bf16[1,128,128]{2,1,0:T(8,128)(2,1)S(1)}) custom-call(bf16[8,1024,128]{2,1,0:T(8,128)(2,1)} %bitcast.7, bf16[8,1024,128]{2,1,0:T(8,128)(2,1)} %bitcast.8, f32[64,4096]{1,0:T(8,128)} %bitcast.9), custom_call_target="tpu_custom_call" | custom-call | tf_op jit(solution)/shard_map/pallas_call | solution.py:229
  49.3 2.1 %shard_map.67 = (bf16[1,8192,128]{2,1,0:T(8,128)(2,1)}, bf16[1,8192,128]{2,1,0:T(8,128)(2,1)}, bf16[1,128,128]{2,1,0:T(8,128)(2,1)}, bf16[1,128,128]{2,1,0:T(8,128)(2,1)}) custom-call(bf16[1,8192,128]{2,1,0:T(8,128)(2,1)S(1)} %get-tuple-element.12.refs_0_, bf16[1,8192,128]{2,1,0:T(8,128)(2,1)S(1)} %get-tuple-element.13.refs_1_, ...), custom_call_target="tpu_custom_call" | custom-call | tf_op jit(solution)/shard_map/pallas_call | solution.py:261

commit v2 on v1

--- a/solution.py
+++ b/solution.py
@@ -10,10 +10,13 @@
 PAGE = 64
 MESH = pl.DeviceIdType.MESH
 
-FIRST = (("YX", "kv"),)
-EVEN = (("Dd", "kv"), ("Yy", "kv"), ("c", "k"), ("Xx", "kv"), ("c", "v"))
-ODD = (("xy", "kv"), ("c", "k"), ("Dd", "kv"), ("c", "v"))
-TURNS = "YXDdxyc"
+FIRST = (("YX", "k"),)
+EVEN = (("dy", "kv"), ("c", "k"), ("xY", "kv"), ("D", "kv"), ("X", "kv"), ("c", "v"))
+ODD = (("xy", "v"), ("c", "k"), ("D", "k"), ("d", "kv"), ("c", "v"))
+MIDDLE = (("xy", "k"),)
+LAST = (("DYX", "v"),)
+ALL = (("cXYxy", "k"), ("cXYxy", "v"), ("Dd", "k"), ("Dd", "v"))
+TURNS = "dYyXxDc"
 
 
 def offsets(outer, inner):
@@ -27,6 +30,11 @@
         if (do, dx, dc) != (0, 0, 0)
     ]
     return cores, chips, steps
+
+
+def is_square(outer, inner):
+    cores, chips, _ = offsets(outer, inner)
+    return (outer, chips, cores) == (2, 2, 2)
 
 
 def kind(step):
@@ -77,7 +85,7 @@
                     sem, inc=1, device_id={"outer": po, "inner": pi}, device_id_type=MESH
                 )
 
-    square = (outer, chips, cores) == (2, 2, 2)
+    square = is_square(outer, inner)
     barrier = pltpu.get_barrier_semaphore()
     if square:
         pl.when((c == 1) & (o + x < 2))(lambda: tell(barrier, "XY"))
@@ -140,6 +148,8 @@
             for stage in (2, 3):
                 tell(ready.at[stage], "XY")
                 pl.semaphore_wait(ready.at[stage], 2)
+                if stage == 2:
+                    issue(MIDDLE)
             tell(ready.at[1], "c")
 
         @pl.when(c == 0)
@@ -148,13 +158,15 @@
             pl.semaphore_wait(ready.at[1], 1)
     else:
         pl.semaphore_wait(barrier, len(steps))
-        pl.when(c == 1)(lambda: issue(FIRST))
 
     get_angles.start()
     own_keys.start()
     own_values.start()
-    pl.when(c == 0)(lambda: issue(EVEN))
-    pl.when(c == 1)(lambda: issue(ODD))
+    if square:
+        pl.when(c == 0)(lambda: issue(EVEN))
+        pl.when(c == 1)(lambda: issue(ODD))
+    else:
+        issue(ALL)
 
     get_angles.wait()
 
@@ -198,26 +210,125 @@
         po, pi = partner(steps[j], -1)
         turn(po * inner + pi)
     own_values.wait()
-    for j in range(len(steps)):
-        copies[j, "v"].wait_recv()
-    for copy in copies.values():
-        copy.wait_send()
+    late = queue(steps, LAST) if square else []
+    sent = [n for n in copies if n not in late]
+    for j, tensor in sent:
+        if tensor == "v":
+            copies[j, tensor].wait_recv()
+    for n in sent:
+        copies[n].wait_send()
+
+    @pl.when(c == 0)
+    def _():
+        for n in late:
+            copies[n].wait_recv()
+            copies[n].wait_send()
+
+
+def last_kernel(outer, inner, values, after, arrived, send, recv):
+    own = arrived.shape[1]
+    cores, chips, steps = offsets(outer, inner)
+    o, i = lax.axis_index("outer"), lax.axis_index("inner")
+    x, c = i // cores, i % cores
+    targets = []
+    for j, _ in queue(steps, LAST):
+        do, dx, dc = steps[j]
+        targets.append(((o + do) % outer, (x + dx) % chips * cores + c))
+
+    @pl.when(c == 1)
+    def _():
+        barrier = pltpu.get_barrier_semaphore()
+        for po, pi in targets:
+            pl.semaphore_signal(
+                barrier, inc=1, device_id={"outer": po, "inner": pi}, device_id_type=MESH
+            )
+        pl.semaphore_wait(barrier, len(targets))
+        copies = [
+            pltpu.make_async_remote_copy(
+                src_ref=values.at[pl.ds((po * inner + pi) * own, own)],
+                dst_ref=arrived.at[n],
+                send_sem=send.at[n],
+                recv_sem=recv.at[n],
+                device_id={"outer": po, "inner": pi},
+                device_id_type=MESH,
+            )
+            for n, (po, pi) in enumerate(targets)
+        ]
+        for copy in copies:
+            copy.start()
+        for copy in copies:
+            copy.wait()
 
 
 def in_hbm(array):
     return pltpu.with_memory_space_constraint(array, pltpu.HBM)
 
 
-def store(*refs):
+def store(outer, inner, *refs):
     count = len(refs) // 2
     sems = refs[-1]
-    copies = [
-        pltpu.make_async_copy(refs[k], refs[count + k], sems.at[k]) for k in range(count)
+    square = is_square(outer, inner)
+    always = [
+        pltpu.make_async_copy(refs[k], refs[count + k], sems.at[k])
+        for k in range(count)
+        if k != 1 or not square
     ]
-    for copy in copies:
+    if not square:
+        for copy in always:
+            copy.start()
+        for copy in always:
+            copy.wait()
+        return
+
+    group = outer * inner
+    rows = refs[1].shape[1] // group
+    o, i = lax.axis_index("outer"), lax.axis_index("inner")
+    x, c = i // 2, i % 2
+    steps = offsets(outer, inner)[2]
+    waiting = [steps[j] for j, _ in queue(steps, LAST)]
+    parts = []
+    for do, dx, dc in [(0, 0, 0)] + steps:
+        origin = (o + do) % 2 * inner + (x + dx) % 2 * 2 + (c + dc) % 2
+        at = pl.ds(pl.multiple_of(origin * rows, rows), rows)
+        late = (do, dx, dc) in waiting
+        parts.append((late, pltpu.make_async_copy(
+            refs[1].at[:, at], refs[count + 1].at[:, at], sems.at[count + len(parts)]
+        )))
+    always += [copy for late, copy in parts if not late]
+    for copy in always:
         copy.start()
-    for copy in copies:
+
+    @pl.when(c == 0)
+    def _():
+        for late, copy in parts:
+            if late:
+                copy.start()
+        for late, copy in parts:
+            if late:
+                copy.wait()
+
+    for copy in always:
         copy.wait()
+
+
+def store_last(outer, inner, arrived, before, values, sems):
+    rows = arrived.shape[2]
+    o, i = lax.axis_index("outer"), lax.axis_index("inner")
+    x, c = i // 2, i % 2
+
+    @pl.when(c == 1)
+    def _():
+        copies = []
+        steps = offsets(outer, inner)[2]
+        for n, (j, _) in enumerate(queue(steps, LAST)):
+            do, dx, dc = steps[j]
+            origin = (o + do) % 2 * inner + (x + dx) % 2 * 2 + c
+            at = pl.ds(pl.multiple_of(origin * rows, rows), rows)
+            copies.append(pltpu.make_async_copy(arrived.at[n], values.at[:, at], sems.at[n]))
+        for copy in copies:
+            copy.start()
+        for copy in copies:
+            copy.wait()
 
 
 def per_device(outer, inner, raw_keys, raw_values, turn_angle):
@@ -259,13 +370,37 @@
         in_hbm(turn_angle.T),
     )
     keys, values, high, low = pl.pallas_call(
-        store,
-        out_shape=[jax.ShapeDtypeStruct(out.shape, out.dtype) for out in outs],
+        functools.partial(store, outer, inner),
+        out_shape=[pltpu.HBM(out.shape, out.dtype) for out in outs],
         in_specs=[pl.BlockSpec(memory_space=pltpu.VMEM)] * 4,
         out_specs=[pl.BlockSpec(memory_space=pltpu.HBM)] * 4,
-        scratch_shapes=[pltpu.SemaphoreType.DMA((4,))],
+        scratch_shapes=[pltpu.SemaphoreType.DMA((4 + group,))],
         compiler_params=pltpu.CompilerParams(vmem_limit_bytes=2**20),
     )(*outs)
+    if is_square(outer, inner):
+        late = len(queue(offsets(outer, inner)[2], LAST))
+        arrived = pl.pallas_call(
+            functools.partial(last_kernel, outer, inner),
+            out_shape=pltpu.VMEM((late, own, rows, size), bf16),
+            in_specs=[pl.BlockSpec(memory_space=pltpu.HBM)] * 2,
+            out_specs=pl.BlockSpec(memory_space=pltpu.VMEM),
+            scratch_shapes=[pltpu.SemaphoreType.DMA((late,))] * 2,
+            compiler_params=pltpu.CompilerParams(
+                collective_id=1, has_side_effects=True, vmem_limit_bytes=2**20 + late * own * rows * size * 2
+            ),
+        )(in_hbm(raw_values.reshape(batch, rows, size)), in_hbm(low))
+        values = pl.pallas_call(
+            functools.partial(store_last, outer, inner),
+            out_shape=pltpu.HBM(values.shape, values.dtype),
+            in_specs=[
+                pl.BlockSpec(memory_space=pltpu.VMEM),
+                pl.BlockSpec(memory_space=pltpu.HBM),
+            ],
+            out_specs=pl.BlockSpec(memory_space=pltpu.HBM),
+            scratch_shapes=[pltpu.SemaphoreType.DMA((late,))],
+            input_output_aliases={1: 0},
+            compiler_params=pltpu.CompilerParams(vmem_limit_bytes=2**20),
+        )(arrived, values)
     return (
         keys.reshape(own, group * length, heads, size),
         values.reshape(own, group * length, heads, size),

time: 51.6 us -> 50.8 us (0.984)
  Pallas kernels: 50.8 us -> 50 us
    pallas_call x1, Pallas kernels: 48.7 us -> 37 us  [per_device(): pl.pallas_call(functools.partial(kernel, outer, inner, heads), out_shape=...]
    pallas_call x1 -> x3, Pallas kernels: 2.05 us -> 12.9 us  [the longest x1 10.1 us: per_device(): pl.pallas_call(functools.partial(last_kernel, outer, inner), out_shape=pl...]
where the time goes in v2:
time: 50.8 us; the launch traced here: 50.6 us
  Pallas kernels  50 us (98%)
  between operations  0.65 us (1%)
    pallas_call x1, Pallas kernels, per_device(): pl.pallas_call(functools.partial(kernel, outer, inner, heads), out_shape=...  37 us
    pallas_call x1, Pallas kernels, per_device(): pl.pallas_call(functools.partial(last_kernel, outer, inner), out_shape=pl...  10.1 us
    pallas_call x1, Pallas kernels, per_device(): pl.pallas_call(functools.partial(store, outer, inner), out_shape=[pltpu.H...  1.87 us

profile of v2, /device:TPU:1, one launch (start us, length us, event | category | flops | bytes accessed | tf_op | source)
XLA Modules:
  0.0 50.6 jit_solution(12895286860049535286)
XLA Ops:
  0.6 37.0 %shard_map.66 = (bf16[1,8192,128]{2,1,0:T(8,128)(2,1)S(1)}, bf16[1,8192,128]{2,1,0:T(8,128)(2,1)S(1)}, bf16[1,128,128]{2,1,0:T(8,128)(2,1)S(1)}, bf16[1,128,128]{2,1,0:T(8,128)(2,1)S(1)}) custom-call(bf16[8,1024,128]{2,1,0:T(8,128)(2,1)} %bitcast.9, bf16[8,1024,128]{2,1,0:T(8,128)(2,1)} %bitcast.7, f32[64,4096]{1,0:T(8,128)} %bitcast.11), custom_call_target="tpu_custom_call" | custom-call | tf_op jit(solution)/shard_map/pallas_call | solution.py:340
  37.7 1.9 %shard_map.67 = (bf16[1,8192,128]{2,1,0:T(8,128)(2,1)}, bf16[1,8192,128]{2,1,0:T(8,128)(2,1)}, bf16[1,128,128]{2,1,0:T(8,128)(2,1)}, bf16[1,128,128]{2,1,0:T(8,128)(2,1)}) custom-call(bf16[1,8192,128]{2,1,0:T(8,128)(2,1)S(1)} %get-tuple-element.12.refs_0_, bf16[1,8192,128]{2,1,0:T(8,128)(2,1)S(1)} %get-tuple-element.13.refs_1_, ...), custom_call_target="tpu_custom_call" | custom-call | tf_op jit(solution)/shard_map/pallas_call | solution.py:372
  39.6 10.1 %shard_map.68.arrived = bf16[3,1,1024,128]{3,2,1,0:T(8,128)(2,1)S(1)} custom-call(bf16[8,1024,128]{2,1,0:T(8,128)(2,1)} %bitcast.8, bf16[1,128,128]{2,1,0:T(8,128)(2,1)} %get-tuple-element.17.after), custom_call_target="tpu_custom_call" | custom-call | tf_op jit(solution)/shard_map/pallas_call | solution.py:382
  49.7 0.9 %shard_map.69 = bf16[1,8192,128]{2,1,0:T(8,128)(2,1)} custom-call(bf16[3,1,1024,128]{3,2,1,0:T(8,128)(2,1)S(1)} %shard_map.68.arrived, bf16[1,8192,128]{2,1,0:T(8,128)(2,1)} %get-tuple-element.18.before), custom_call_target="tpu_custom_call", output_to_operand_aliasing={{}: (1, {})} | custom-call | tf_op jit(solution)/shard_map/pallas_call | solution.py:392
